TPU v7x, 32 devices: a whole 2x2x4 slice. The times are simulated.
32 devices in a mesh: slab: 4 (over z), tile: 8 (over y, x, core).
Axes of the slice: x: 2, y: 2, z: 4, core: 2. Of those that a mesh axis runs over, the one named last changes fastest.
Arguments:
- voxel_grid: float32 [4, 64, 64, 256], P(None, 'slab', 'tile'), may hold values from -4 to 4
- first_moment: float32 [4, 64, 64, 256], P(None, 'slab', 'tile'), may hold values from -0.75 to 0.75
- second_moment: float32 [4, 64, 64, 256], P(None, 'slab', 'tile'), may hold values from 0.01 to 0.5
- pixel_index: int32 [32768], P('tile'), may hold values from 0 to 2047
- start_slab: int32 [32768], P('tile'), may hold values from 0 to 1
- ray_count: int32 [32768], P('tile'), may hold values from 16 to 48
- target: float32 [3, 32768], P(None, 'tile'), may hold values from 0 to 1
Outputs:
- new_grid: float32 [4, 64, 64, 256], P(None, 'slab', 'tile')
- new_first: float32 [4, 64, 64, 256], P(None, 'slab', 'tile')
- new_second: float32 [4, 64, 64, 256], P(None, 'slab', 'tile')
All inputs are finite; a program needn't handle non-finite values.
Results may differ from a plain program's by a relative error of at most 0.0003.
Values sent between devices are 32-bit elements; how exact they have to be, the bound alone decides.
A program may use at most 128 MiB of HBM per device.

v0:
```python
import math

import jax
import jax.numpy as jnp
from jax import lax
from jax.sharding import PartitionSpec as P

STEP = 20


RENDER_WEIGHT = 1000.0
TV_WEIGHT = 0.05
BACKGROUND = 1.0
STEP_SPAN = 4.0
CLIP_RMS = 0.25
LEARN_RATE = 0.02
BETA_ONE = 0.9
BETA_TWO = 0.99
EPSILON = 1e-08
BLOCK_LIMIT = 1024


def padded_2(cells, sides, width):
    for axis, dim in sides:
        count = lax.axis_size(axis)
        ends = count - 1
        head = lax.slice_in_dim(cells, 0, width, axis=dim)
        tail = lax.slice_in_dim(cells, cells.shape[dim] - width, cells.shape[dim], axis=dim)
        cells = jnp.concatenate(
            [
                lax.ppermute(tail, axis, [(i, (i + 1) % count) for i in range(ends)]),
                cells,
                lax.ppermute(head, axis, [((i + 1) % count, i) for i in range(ends)]),
            ],
            axis=dim,
        )
    return cells


def carried_in(part, axis, combine, identity, reverse):
    count = lax.axis_size(axis)
    place = lax.axis_index(axis)
    ahead = count - 1 - place if reverse else place
    gathered = jax.tree.map(lambda a: lax.all_gather(a, axis), part)
    state = jax.tree.map(lambda a, e: jnp.zeros_like(a) + jnp.asarray(e, a.dtype), part, identity)

    def one(step, state):
        source = count - 1 - step if reverse else step
        return combine(
            state, jax.tree.map(lambda a: lax.dynamic_index_in_dim(a, source, 0, False), gathered)
        )

    return lax.fori_loop(0, ahead, one, state)


def front_join(earlier, later):
    return (earlier[0] + earlier[1][None] * later[0], earlier[1] * later[1])


def back_join(earlier, later):
    return (later[0] + later[1][None] * earlier[0], later[1] * earlier[1])


def per_device(voxel_grid, first_moment, second_moment, pixel_index, start_slab, ray_count, target):
    slab_count = lax.axis_size("slab")
    tile_count = lax.axis_size("tile")
    slab_pos = lax.axis_index("slab")
    tile_pos = lax.axis_index("tile")
    channels, slab_depth, rows_x, rows_y = voxel_grid.shape
    total_depth = slab_depth * slab_count
    total_x = rows_x * tile_count
    pixel_total = rows_x * rows_y
    ray_total = pixel_index.shape[0]
    ray_block = math.gcd(ray_total, BLOCK_LIMIT)
    block_count = ray_total // ray_block
    padded = padded_2(voxel_grid, (("slab", 1), ("tile", 2)), 1)
    depth_pos = slab_pos * slab_depth + jnp.arange(slab_depth, dtype=jnp.int32)
    first_cell = start_slab[None, :] * (total_depth // slab_count)
    inside = (depth_pos[:, None] >= first_cell) & (
        depth_pos[:, None] < first_cell + ray_count[None, :]
    )
    pixel_blocks = pixel_index.reshape(block_count, ray_block)
    pixel_ids = jnp.arange(pixel_total, dtype=jnp.int32)
    depth_ids = jnp.arange(slab_depth, dtype=jnp.int32)
    lower = (depth_ids[:, None] >= depth_ids[None, :]).astype(jnp.float32)

    def march_slab(local_grid):
        flat = local_grid.reshape(channels * slab_depth, pixel_total)

        def pick_block(block_pixels):
            selector = (pixel_ids[:, None] == block_pixels[None, :]).astype(jnp.float32)
            return jnp.dot(
                flat, selector, precision=lax.Precision.HIGHEST, preferred_element_type=jnp.float32
            )

        picked = lax.map(pick_block, pixel_blocks)
        samples = picked.transpose(1, 0, 2).reshape(channels, slab_depth, ray_total)
        optical = jnp.where(inside, jax.nn.softplus(samples[0]) * (STEP_SPAN / total_depth), 0.0)
        running = jnp.dot(
            lower, optical, precision=lax.Precision.HIGHEST, preferred_element_type=jnp.float32
        )
        weights = jnp.exp(-(running - optical)) * (1.0 - jnp.exp(-optical))
        colors = jax.nn.sigmoid(samples[1:4])
        return (jnp.sum(weights[None] * colors, axis=1), jnp.exp(-running[-1]))

    (part_color, part_trans), pullback = jax.vjp(march_slab, voxel_grid)
    empty = (jnp.zeros_like(part_color), jnp.ones_like(part_trans))
    front_color, front_trans = carried_in(
        (part_color, part_trans), "slab", front_join, empty, False
    )
    back_color, back_trans = carried_in((part_color, part_trans), "slab", back_join, empty, True)
    beyond = back_color + back_trans[None] * BACKGROUND
    rendered = front_color + front_trans[None] * (part_color + part_trans[None] * beyond)
    residual = RENDER_WEIGHT * (rendered - target)
    color_cot = front_trans[None] * residual
    trans_cot = front_trans * jnp.sum(residual * beyond, axis=0)
    render_grad = pullback((color_cot, trans_cot))[0]
    depth_view = depth_pos.reshape(1, slab_depth, 1, 1)
    x_view = (tile_pos * rows_x + jnp.arange(rows_x, dtype=jnp.int32)).reshape(1, 1, rows_x, 1)
    smooth = jnp.where(depth_view > 0, voxel_grid - padded[:, :-2, 1:-1, :], 0.0)
    smooth = smooth + jnp.where(
        depth_view < total_depth - 1, voxel_grid - padded[:, 2:, 1:-1, :], 0.0
    )
    smooth = smooth + jnp.where(x_view > 0, voxel_grid - padded[:, 1:-1, :-2, :], 0.0)
    smooth = smooth + jnp.where(x_view < total_x - 1, voxel_grid - padded[:, 1:-1, 2:, :], 0.0)
    step_y = jnp.diff(voxel_grid, axis=3)
    smooth = (
        smooth
        + jnp.pad(-step_y, ((0, 0), (0, 0), (0, 0), (0, 1)))
        + jnp.pad(step_y, ((0, 0), (0, 0), (0, 0), (1, 0)))
    )
    gradient = render_grad + 2.0 * TV_WEIGHT * smooth
    square_sum = lax.psum(jnp.sum(gradient * gradient), ("slab", "tile"))
    norm_value = jnp.sqrt(square_sum)
    limit = CLIP_RMS * math.sqrt(4.0 * total_depth * total_x * rows_y)
    clipped = gradient * (limit / jnp.maximum(norm_value, limit))
    new_first = BETA_ONE * first_moment + (1.0 - BETA_ONE) * clipped
    new_second = BETA_TWO * second_moment + (1.0 - BETA_TWO) * clipped * clipped
    first_hat = new_first / (1.0 - BETA_ONE**STEP)
    second_hat = new_second / (1.0 - BETA_TWO**STEP)
    new_grid = voxel_grid - LEARN_RATE * first_hat / (jnp.sqrt(second_hat) + EPSILON)
    return (new_grid, new_first, new_second)


def solution(mesh):
    placed = (
        P(None, "slab", "tile", None),
        P(None, "slab", "tile", None),
        P(None, "slab", "tile", None),
        P("tile"),
        P("tile"),
        P("tile"),
        P(None, "tile"),
    )
    return jax.shard_map(
        per_device,
        mesh=mesh,
        in_specs=placed,
        out_specs=(
            P(None, "slab", "tile", None),
            P(None, "slab", "tile", None),
            P(None, "slab", "tile", None),
        ),
        check_vma=False,
    )
```

profile of v0, /device:TPU:0, one launch (start us, length us, event | category | flops | bytes accessed | tf_op | source)
XLA Modules:
  0.0 174.9 jit_solution(10069443243071050451)
XLA Ops:
  0.6 0.8 fusion.58
  1.4 4.9 %collective-permute-start = (f32[4,1,8,256]{3,2,1,0:T(8,128)S(1)}, f32[4,1,8,256]{3,2,1,0:T(8,128)S(1)}, u32[]{:S(2)}, u32[]{:S(2)}) collective-permute-start(f32[4,1,8,256]{3,2,1,0:T(8,128)S(1)} %get-tuple-element.347), channel_id=1, source_target_pairs={{0,8},{8,16},{16,24},{1,9},{9,17},{17,25},{2,10},{10,18},{18,26},{... | collective-permute-start | bytes 98312 | tf_op jit(solution)/shard_map/ppermute | solution.py:31
  6.4 1.3 collective-permute-start.1
  7.7 1.2 copy.45
  8.9 0.7 reshape.125
  9.6 0.0 copy-start
  9.6 30.4 %while.57 = (s32[]{:T(128)}, f32[4,64,1024]{2,1,0:T(8,128)S(1)}, f32[4,2048,1024]{2,1,0:T(8,128)}, s32[4,1024]{1,0:T(4,128)S(1)}, f32[64,2048]{1,0:T(8,128)S(1)}, /*index=5*/s32[]{:T(128)}) while((s32[]{:T(128)}, f32[4,64,1024]{2,1,0:T(8,128)S(1)}, f32[4,2048,1024]{2,1,0:T(8,128)}, s32[4,1024]{1,0:T(4,128)S(1)}, ...), condition=%wide.region_1.2_spmd.clone.clone, body=%wide.region_0.1_spmd.clone.clone.sunk | while | flops 1616904192 | bytes 9192013 | solution.py:96
  9.7 3.1 %fusion.69 = f32[4,64,1024]{2,1,0:T(8,128)S(1)} fusion(f32[4,64,1024]{2,1,0:T(8,128)S(1)} %get-tuple-element.495, s32[]{:T(128)} %get-tuple-element.494, f32[64,2048]{1,0:T(8,128)S(1)} %get-tuple-element.504, s32[1024]{0:T(1024)S(1)} %bitcast.79), kind=kOutput, calls=%fused_computation.12.clone.1 | convolution fusion | flops 1612709888 | bytes 790532 | tf_op jit(solution)/shard_map/jvp()/while/body/eval_jaxpr/dot_general | solution.py:92
  12.8 4.5 %convert_dynamic-update-slice_fusion.2 = f32[4,2048,1024]{2,1,0:T(8,128)} fusion(f32[4,2048,1024]{2,1,0:T(8,128)} %get-tuple-element.496, s32[]{:T(128)} %get-tuple-element.494, s32[1024]{0:T(1024)S(1)} %bitcast.80), kind=kLoop, calls=%fused_computation.8.clone.1 | loop fusion | flops 4194304 | bytes 8393216 | tf_op jit(solution)/shard_map/jvp()/while/body/jit(dynamic_update_index_in_dim)/dynamic_update_slice | solution.py:96
  17.3 3.1 %fusion.69 = f32[4,64,1024]{2,1,0:T(8,128)S(1)} fusion(f32[4,64,1024]{2,1,0:T(8,128)S(1)} %get-tuple-element.495, s32[]{:T(128)} %get-tuple-element.494, f32[64,2048]{1,0:T(8,128)S(1)} %get-tuple-element.504, s32[1024]{0:T(1024)S(1)} %bitcast.79), kind=kOutput, calls=%fused_computation.12.clone.1 | convolution fusion | flops 1612709888 | bytes 790532 | tf_op jit(solution)/shard_map/jvp()/while/body/eval_jaxpr/dot_general | solution.py:92
  20.4 4.5 %convert_dynamic-update-slice_fusion.2 = f32[4,2048,1024]{2,1,0:T(8,128)} fusion(f32[4,2048,1024]{2,1,0:T(8,128)} %get-tuple-element.496, s32[]{:T(128)} %get-tuple-element.494, s32[1024]{0:T(1024)S(1)} %bitcast.80), kind=kLoop, calls=%fused_computation.8.clone.1 | loop fusion | flops 4194304 | bytes 8393216 | tf_op jit(solution)/shard_map/jvp()/while/body/jit(dynamic_update_index_in_dim)/dynamic_update_slice | solution.py:96
  24.9 3.1 %fusion.69 = f32[4,64,1024]{2,1,0:T(8,128)S(1)} fusion(f32[4,64,1024]{2,1,0:T(8,128)S(1)} %get-tuple-element.495, s32[]{:T(128)} %get-tuple-element.494, f32[64,2048]{1,0:T(8,128)S(1)} %get-tuple-element.504, s32[1024]{0:T(1024)S(1)} %bitcast.79), kind=kOutput, calls=%fused_computation.12.clone.1 | convolution fusion | flops 1612709888 | bytes 790532 | tf_op jit(solution)/shard_map/jvp()/while/body/eval_jaxpr/dot_general | solution.py:92
  28.0 4.5 %convert_dynamic-update-slice_fusion.2 = f32[4,2048,1024]{2,1,0:T(8,128)} fusion(f32[4,2048,1024]{2,1,0:T(8,128)} %get-tuple-element.496, s32[]{:T(128)} %get-tuple-element.494, s32[1024]{0:T(1024)S(1)} %bitcast.80), kind=kLoop, calls=%fused_computation.8.clone.1 | loop fusion | flops 4194304 | bytes 8393216 | tf_op jit(solution)/shard_map/jvp()/while/body/jit(dynamic_update_index_in_dim)/dynamic_update_slice | solution.py:96
  32.5 3.1 %fusion.69 = f32[4,64,1024]{2,1,0:T(8,128)S(1)} fusion(f32[4,64,1024]{2,1,0:T(8,128)S(1)} %get-tuple-element.495, s32[]{:T(128)} %get-tuple-element.494, f32[64,2048]{1,0:T(8,128)S(1)} %get-tuple-element.504, s32[1024]{0:T(1024)S(1)} %bitcast.79), kind=kOutput, calls=%fused_computation.12.clone.1 | convolution fusion | flops 1612709888 | bytes 790532 | tf_op jit(solution)/shard_map/jvp()/while/body/eval_jaxpr/dot_general | solution.py:92
  35.6 4.5 %convert_dynamic-update-slice_fusion.2 = f32[4,2048,1024]{2,1,0:T(8,128)} fusion(f32[4,2048,1024]{2,1,0:T(8,128)} %get-tuple-element.496, s32[]{:T(128)} %get-tuple-element.494, s32[1024]{0:T(1024)S(1)} %bitcast.80), kind=kLoop, calls=%fused_computation.8.clone.1 | loop fusion | flops 4194304 | bytes 8393216 | tf_op jit(solution)/shard_map/jvp()/while/body/jit(dynamic_update_index_in_dim)/dynamic_update_slice | solution.py:96
  40.1 0.2 fusion.23
  40.4 1.3 subtract_multiply_fusion.1
  41.7 0.9 fusion.60
  42.6 0.9 fusion.48
  43.6 1.2 fusion.56
  44.8 0.5 copy.37
  45.3 0.5 div.21
  45.8 0.2 multiply_reduce_fusion.1
  46.0 15.2 %all-gather.1 = f32[4,3,4096]{2,1,0:T(4,128)S(1)} all-gather(f32[1,3,4096]{2,1,0:T(4,128)S(1)} %bitcast.77), channel_id=2, replica_groups=mesh['slab'=4,'tile'=8] {'slab'}, dimensions={0}, use_global_device_ids=true | all-gather | bytes 245760 | tf_op jit(solution)/shard_map/all_gather | solution.py:44
  61.2 13.1 %all-gather.2 = f32[4,1,4096]{2,1,0:T(1,128)S(1)} all-gather(f32[1,1,4096]{2,1,0:T(1,128)S(1)} %fusion.60), channel_id=1, replica_groups=mesh['slab'=4,'tile'=8] {'slab'}, dimensions={0}, use_global_device_ids=true | all-gather | bytes 81920 | tf_op jit(solution)/shard_map/all_gather | solution.py:44
  74.4 0.5 while.56
  74.9 0.1 broadcast_multiply_fusion
  75.0 0.2 fusion.20
  75.2 0.1 multiply_reduce_fusion.3
  75.3 1.9 %fusion.19 = f32[1,16,4096]{2,1,0:T(8,128)S(1)} fusion(f32[16,4096]{1,0:T(8,128)S(1)} %bitcast.82, f32[1,4096]{1,0:T(1,128)S(1)} %bitcast.85, f32[16,4096]{1,0:T(8,128)S(1)} %get-tuple-element.343, s32[4096]{0:T(1024)S(1)} %get-tuple-element.349, s32[4096]{0:T(1024)S(1)} %get-tuple-element.348, s32[16]{0:T(128)S(1)} %iota_add_fusion.1, ...), kind=kOutput, calls=%fused_computation.25 | convolution fusion | flops 15859968 | bytes 1097792 | tf_op jit(solution)/shard_map/transpose(jvp())/dot_general | solution.py:99
  77.1 0.1 pad_add_fusion
  77.2 0.7 reshape.127
  77.9 0.6 copy.49
  78.6 41.8 %while.58 = (s32[]{:T(128)}, f32[64,2048]{1,0:T(8,128)S(1)}, f32[4,64,1024]{2,1,0:T(8,128)S(1)}, f32[4,2048,1024]{2,1,0:T(8,128)}, s32[]{:T(128)}, /*index=5*/s32[]{:T(128)}, s32[]{:T(128)}) while((s32[]{:T(128)}, f32[64,2048]{1,0:T(8,128)S(1)}, f32[4,64,1024]{2,1,0:T(8,128)S(1)}, f32[4,2048,1024]{2,1,0:T(8,128)}, s32[]{:T(128)}, ...), condition=%wide.region_10.11_spmd.clone, body=%wide.region_9.10_spmd.clone.sunk | while | flops 1610874880 | bytes 9700962 | solution.py:96
  78.6 10.5 %fusion.72 = f32[64,2048]{1,0:T(8,128)S(1)} fusion(f32[4,2048,1024]{2,1,0:T(8,128)} %get-tuple-element.580, s32[]{:T(128)S(6)} %sub.139, f32[64,2048]{1,0:T(8,128)S(1)} %get-tuple-element.571, f32[4,64,1024]{2,1,0:T(8,128)S(1)} %get-tuple-element.579, pred[]{:T(512)S(6)} %compare.8), kind=kOutput, calls=%fused_computation.17.clone.1 | convolution fusion | flops 1610874880 | bytes 9700864 | tf_op jit(solution)/shard_map/transpose(jvp())/while/body/eval_jaxpr/dot_general | solution.py:92
  89.1 10.4 %fusion.72 = f32[64,2048]{1,0:T(8,128)S(1)} fusion(f32[4,2048,1024]{2,1,0:T(8,128)} %get-tuple-element.580, s32[]{:T(128)S(6)} %sub.139, f32[64,2048]{1,0:T(8,128)S(1)} %get-tuple-element.571, f32[4,64,1024]{2,1,0:T(8,128)S(1)} %get-tuple-element.579, pred[]{:T(512)S(6)} %compare.8), kind=kOutput, calls=%fused_computation.17.clone.1 | convolution fusion | flops 1610874880 | bytes 9700864 | tf_op jit(solution)/shard_map/transpose(jvp())/while/body/eval_jaxpr/dot_general | solution.py:92
  99.5 10.4 %fusion.72 = f32[64,2048]{1,0:T(8,128)S(1)} fusion(f32[4,2048,1024]{2,1,0:T(8,128)} %get-tuple-element.580, s32[]{:T(128)S(6)} %sub.139, f32[64,2048]{1,0:T(8,128)S(1)} %get-tuple-element.571, f32[4,64,1024]{2,1,0:T(8,128)S(1)} %get-tuple-element.579, pred[]{:T(512)S(6)} %compare.8), kind=kOutput, calls=%fused_computation.17.clone.1 | convolution fusion | flops 1610874880 | bytes 9700864 | tf_op jit(solution)/shard_map/transpose(jvp())/while/body/eval_jaxpr/dot_general | solution.py:92
  109.9 10.4 %fusion.72 = f32[64,2048]{1,0:T(8,128)S(1)} fusion(f32[4,2048,1024]{2,1,0:T(8,128)} %get-tuple-element.580, s32[]{:T(128)S(6)} %sub.139, f32[64,2048]{1,0:T(8,128)S(1)} %get-tuple-element.571, f32[4,64,1024]{2,1,0:T(8,128)S(1)} %get-tuple-element.579, pred[]{:T(512)S(6)} %compare.8), kind=kOutput, calls=%fused_computation.17.clone.1 | convolution fusion | flops 1610874880 | bytes 9700864 | tf_op jit(solution)/shard_map/transpose(jvp())/while/body/eval_jaxpr/dot_general | solution.py:92
  120.4 0.2 copy.46
  120.6 0.1 fusion.57
  120.8 1.3 collective-permute-start.2
  122.1 1.3 collective-permute-start.3
  123.4 0.1 copy.40
  123.5 3.4 %collective-permute-done.3 = f32[4,18,1,256]{3,1,2,0:T(8,128)S(1)} collective-permute-done((f32[4,18,1,256]{3,1,2,0:T(8,128)S(1)}, f32[4,18,1,256]{3,1,2,0:T(8,128)S(1)}, u32[]{:S(2)}, u32[]{:S(2)}) %collective-permute-start.3) | collective-permute-done | bytes 73760 | tf_op jit(solution)/shard_map/ppermute | solution.py:33
  126.9 0.1 copy.42
  127.0 1.2 multiply_reduce_fusion.2
  128.2 43.4 %psum.7 = f32[]{:T(128)} all-reduce(f32[]{:T(128)} %get-tuple-element.336), channel_id=1, replica_groups=mesh['slab'=4,'tile'=8] {'slab','tile'}, use_global_device_ids=true, to_apply=%region_12.13 | all-reduce | flops 1 | bytes 8 | tf_op jit(solution)/shard_map/psum | solution.py:133
  172.4 2.5 %divide_subtract_fusion = (f32[4,16,8,256]{3,2,1,0:T(8,128)}, f32[4,16,8,256]{3,2,1,0:T(8,128)}, f32[4,16,8,256]{3,2,1,0:T(8,128)}) fusion(f32[4,16,8,256]{3,2,1,0:T(8,128)S(1)} %copy-done, f32[4,16,8,256]{3,2,1,0:T(8,128)S(1)} %get-tuple-element.337, f32[]{:T(128)S(6)} %div.22, f32[4,16,8,256]{3,2,1,0:T(8,128)} %param.16, f32[4,16,8,256]{3,2,1,0:T(8,128)} %param.17), kind=kLoop, calls=%fused_computation.60 | loop fusion | flops 1703936 | bytes 3670020 | tf_op jit(solution)/shard_map/sub | solution.py:141
  (49 shorter events, 0.5 us)
Async XLA Ops:
  1.4 119.1 %collective-permute-start = (f32[4,1,8,256]{3,2,1,0:T(8,128)S(1)}, f32[4,1,8,256]{3,2,1,0:T(8,128)S(1)}, u32[]{:S(2)}, u32[]{:S(2)}) collective-permute-start(f32[4,1,8,256]{3,2,1,0:T(8,128)S(1)} %get-tuple-element.347), channel_id=1, source_target_pairs={{0,8},{8,16},{16,24},{1,9},{9,17},{17,25},{2,10},{10,18},{18,26},{... | collective-permute-start | bytes 98312 | tf_op jit(solution)/shard_map/ppermute | solution.py:31
  6.4 114.3 %collective-permute-start.1 = (f32[4,1,8,256]{3,2,1,0:T(8,128)S(1)}, f32[4,1,8,256]{3,2,1,0:T(8,128)S(1)}, u32[]{:S(2)}, u32[]{:S(2)}) collective-permute-start(f32[4,1,8,256]{3,2,1,0:T(8,128)S(1)} %get-tuple-element.346), channel_id=1, source_target_pairs={{8,0},{16,8},{24,16},{9,1},{17,9},{25,17},{10,2},{18,10},{26,18},{... | collective-permute-start | bytes 98312 | tf_op jit(solution)/shard_map/ppermute | solution.py:33
  9.6 30.7 %copy-start.4 = (s32[4096]{0:T(1024)S(1)}, s32[4096]{0:T(1024)}, u32[]{:S(2)}) copy-start(s32[4096]{0:T(1024)} %param.19) | copy-start | bytes 49156
  9.6 30.7 %copy-start.5 = (s32[4096]{0:T(1024)S(1)}, s32[4096]{0:T(1024)}, u32[]{:S(2)}) copy-start(s32[4096]{0:T(1024)} %param.20) | copy-start | bytes 49156
  9.6 33.9 %copy-start = (f32[4,16,8,256]{3,2,1,0:T(8,128)S(1)}, f32[4,16,8,256]{3,2,1,0:T(8,128)}, u32[]{:S(2)}) copy-start(f32[4,16,8,256]{3,2,1,0:T(8,128)} %param.15) | copy-start | bytes 1572868
  40.1 34.9 %copy-start.3 = (f32[3,4096]{1,0:T(4,128)S(1)}, f32[3,4096]{1,0:T(4,128)}, u32[]{:S(2)}) copy-start(f32[3,4096]{1,0:T(4,128)} %param.21) | copy-start | bytes 147460
  78.6 48.5 %copy-start.1 = (f32[4,16,8,255]{3,2,1,0:T(8,128)S(1)}, f32[4,16,8,255]{3,2,1,0:T(8,128)}, u32[]{:S(2)}) copy-start(f32[4,16,8,255]{3,2,1,0:T(8,128)} %get-tuple-element.338) | copy-start | bytes 1566724
  78.6 48.5 %copy-start.2 = (f32[4,16,8,255]{3,2,1,0:T(8,128)S(1)}, f32[4,16,8,255]{3,2,1,0:T(8,128)}, u32[]{:S(2)}) copy-start(f32[4,16,8,255]{3,2,1,0:T(8,128)} %get-tuple-element.339) | copy-start | bytes 1566724
  120.8 2.6 %collective-permute-start.2 = (f32[4,18,1,256]{3,1,2,0:T(8,128)S(1)}, f32[4,18,1,256]{3,1,2,0:T(8,128)S(1)}, u32[]{:S(2)}, u32[]{:S(2)}) collective-permute-start(f32[4,18,1,256]{3,1,2,0:T(8,128)S(1)} %copy.39), channel_id=1, source_target_pairs={{0,1},{1,2},{2,3},{3,4},{4,5},{5,6},{6,7},{8,9},{9,10},{10,11},{11... | collective-permute-start | bytes 221192 | tf_op jit(solution)/shard_map/ppermute | solution.py:31
  122.1 4.9 %collective-permute-start.3 = (f32[4,18,1,256]{3,1,2,0:T(8,128)S(1)}, f32[4,18,1,256]{3,1,2,0:T(8,128)S(1)}, u32[]{:S(2)}, u32[]{:S(2)}) collective-permute-start(f32[4,18,1,256]{3,1,2,0:T(8,128)S(1)} %copy.41), channel_id=1, source_target_pairs={{1,0},{2,1},{3,2},{4,3},{5,4},{6,5},{7,6},{9,8},{10,9},{11,10},{12... | collective-permute-start | bytes 221192 | tf_op jit(solution)/shard_map/ppermute | solution.py:33
where the time goes:
time: 175 us
  blocking collectives  71.7 us (41%)
  matrix products  57.4 us (33%)
  other arithmetic  25.5 us (15%)
  starting transfers between devices  8.83 us (5%)
  local copies, waits for them, and re-layouts  5.79 us (3%)
  waiting for transfers between devices  3.45 us (2%)
  between operations  1.79 us (1%)
    dot_general x8, matrix products, pick_block(): jnp.dot(flat, selector, precision=lax.Precision.HIGHEST, preferred_elemen...  54.2 us
    psum x1, blocking collectives, per_device(): square_sum = lax.psum(jnp.sum(gradient * gradient), ('slab', 'tile'))  43.4 us
    all_gather x2, blocking collectives, carried_in(): gathered = jax.tree.map(lambda a: lax.all_gather(a, axis), part)  28.3 us
    dynamic_update_slice x4, other arithmetic, march_slab(): picked = lax.map(pick_block, pixel_blocks)  17.8 us
    ppermute x2, starting transfers between devices, padded_2(): lax.ppermute(tail, axis, [(i, (i + 1) % count) for i in range(ends)])  6.24 us
  transfers between devices with their start and end apart: 4, of which 1 were waited for; matrix products, arithmetic and copies ran while one was open for 48% of the time, Pallas kernels for 0%

commit v1 on v0

v1 whole, which is shorter than its diff:
```python
import functools
import math

import jax
import jax.numpy as jnp
from jax import lax
from jax.experimental import pallas as pl
from jax.experimental.pallas import tpu as pltpu
from jax.sharding import PartitionSpec as P

STEP = 20
RENDER_WEIGHT = 1000.0
TV_WEIGHT = 0.05
BACKGROUND = 1.0
STEP_SPAN = 4.0
CLIP_RMS = 0.25
LEARN_RATE = 0.02
BETA_ONE = 0.9
BETA_TWO = 0.99
EPSILON = 1e-08
CHUNK = 1024
MESH = pl.DeviceIdType.MESH


def kernel(
    ns, nt, chunk,
    grid_ref, pix_ref, start_ref, count_ref, target_ref,
    grad_ref, norm_ref,
    hi_ref, lo_ref, trans_ref, weight_ref, sig_ref, onehot_ref, row_ref, parts_ref, table_ref,
    edge_ref, xhalo_ref, zhalo_ref, nsend_ref, nrecv_ref,
    part_send, part_recv, halo_send, halo_recv, norm_send, norm_recv,
):
    channels, depth, rx, ry = grid_ref.shape
    rays = pix_ref.shape[1]
    chunks = rays // chunk
    total_depth = depth * ns
    span = STEP_SPAN / total_depth
    rows = depth * rx
    slab = lax.axis_index("slab")
    tile = lax.axis_index("tile")

    def slab_peer(d):
        return {"slab": lax.rem(slab + d, ns)}

    def tile_peer(d):
        return {"tile": lax.rem(tile + d, nt)}

    barrier = pltpu.get_barrier_semaphore()
    for d in range(1, ns):
        pl.semaphore_signal(barrier, inc=1, device_id=slab_peer(d), device_id_type=MESH)
    for d in range(1, nt):
        pl.semaphore_signal(barrier, inc=1, device_id=tile_peer(d), device_id_type=MESH)

    edge_ref[0] = grid_ref[:, :, rx - 1, :]
    edge_ref[1] = grid_ref[:, :, 0, :]

    total = jnp.zeros((rx, ry), jnp.float32)
    before = jnp.ones((rx, ry), jnp.float32)
    sums = [jnp.zeros((rx, ry), jnp.float32) for _ in range(3)]
    for z in range(depth):
        s = grid_ref[0, z]
        e = jnp.exp(-jnp.abs(s))
        tau = (jnp.maximum(s, 0.0) + jnp.log1p(e)) * span
        sig_ref[0, z] = jnp.where(s >= 0, 1.0, e) / (1.0 + e)
        total = total + tau
        after = jnp.exp(-total)
        w = before * (1.0 - jnp.exp(-tau))
        before = after
        trans_ref[z] = after
        weight_ref[z] = w
        for c in range(3):
            col = 1.0 / (1.0 + jnp.exp(-grid_ref[c + 1, z]))
            sig_ref[c + 1, z] = col
            sums[c] = sums[c] + w * col
            table_ref[pl.ds(c * rows + z * rx, rx), :] = sums[c]
        table_ref[pl.ds(3 * rows + z * rx, rx), :] = after
    full = table_ref[...]
    high = full.astype(jnp.bfloat16)
    hi_ref[...] = high
    lo_ref[...] = (full - high.astype(jnp.float32)).astype(jnp.bfloat16)

    pl.semaphore_wait(barrier, ns - 1 + nt - 1)

    halos = [
        pltpu.make_async_remote_copy(
            src_ref=grid_ref.at[:, depth - 1], dst_ref=zhalo_ref.at[0],
            send_sem=halo_send.at[0], recv_sem=halo_recv.at[0],
            device_id=slab_peer(1), device_id_type=MESH),
        pltpu.make_async_remote_copy(
            src_ref=grid_ref.at[:, 0], dst_ref=zhalo_ref.at[1],
            send_sem=halo_send.at[1], recv_sem=halo_recv.at[1],
            device_id=slab_peer(ns - 1), device_id_type=MESH),
        pltpu.make_async_remote_copy(
            src_ref=edge_ref.at[0], dst_ref=xhalo_ref.at[0],
            send_sem=halo_send.at[2], recv_sem=halo_recv.at[2],
            device_id=tile_peer(1), device_id_type=MESH),
        pltpu.make_async_remote_copy(
            src_ref=edge_ref.at[1], dst_ref=xhalo_ref.at[1],
            send_sem=halo_send.at[3], recv_sem=halo_recv.at[3],
            device_id=tile_peer(nt - 1), device_id_type=MESH),
    ]

    def part_copy(d, j):
        return pltpu.make_async_remote_copy(
            src_ref=parts_ref.at[slab, j], dst_ref=parts_ref.at[slab, j],
            send_sem=part_send.at[d - 1, j], recv_sem=part_recv.at[d - 1, j],
            device_id=slab_peer(d), device_id_type=MESH)

    def part_wait(d, j):
        source = lax.rem(slab + ns - d, ns)
        pltpu.make_async_remote_copy(
            src_ref=parts_ref.at[source, j], dst_ref=parts_ref.at[source, j],
            send_sem=part_send.at[d - 1, j], recv_sem=part_recv.at[d - 1, j],
            device_id=slab_peer(d), device_id_type=MESH).wait_recv()

    y_ids = lax.broadcasted_iota(jnp.int32, (ry, chunk), 0).astype(jnp.float32).astype(jnp.bfloat16)
    row_ids = lax.broadcasted_iota(jnp.int32, (rows, chunk), 0)

    for j in range(chunks):
        at = pl.ds(j * chunk, chunk)
        pix = pix_ref[:, at]
        start = start_ref[:, at]
        px = pix // ry
        py = (pix - px * ry).astype(jnp.float32).astype(jnp.bfloat16)
        length = jnp.clip((start - slab) * depth + count_ref[:, at], 0, depth)
        length = jnp.where(slab >= start, length, 0)
        row = jnp.where(length > 0, (length - 1) * rx + px, -1)
        row_ref[:, at] = row
        hot = jnp.where(y_ids == py, jnp.ones((), jnp.bfloat16), jnp.zeros((), jnp.bfloat16))
        onehot_ref[:, at] = hot
        mask = row_ids == row
        for c in range(4):
            block = pl.ds(c * rows, rows)
            u = jnp.dot(hi_ref[block, :], hot, preferred_element_type=jnp.float32)
            u = u + jnp.dot(lo_ref[block, :], hot, preferred_element_type=jnp.float32)
            part = jnp.sum(jnp.where(mask, u, 0.0), axis=0, keepdims=True)
            if c == 3:
                part = jnp.where(row < 0, 1.0, part)
            parts_ref[slab, j, pl.ds(c, 1), :] = part
        for d in range(1, ns):
            part_copy(d, j).start()
        if j == 0:
            for h in halos:
                h.start()

    for h in halos:
        h.wait_recv()
    x_ids = lax.broadcasted_iota(jnp.int32, (rx, ry), 0)
    lane_ids = lax.broadcasted_iota(jnp.int32, (rx, ry), 1)
    first_x = tile == 0
    last_x = tile == nt - 1
    for c in range(channels):
        for z in range(depth):
            g = grid_ref[c, z]
            if z > 0:
                below = grid_ref[c, z - 1]
            else:
                below = jnp.where(slab > 0, zhalo_ref[0, c], g)
            if z < depth - 1:
                above = grid_ref[c, z + 1]
            else:
                above = jnp.where(slab < ns - 1, zhalo_ref[1, c], g)
            xl = jnp.broadcast_to(xhalo_ref[0, c, pl.ds(z, 1), :], (rx, ry))
            xh = jnp.broadcast_to(xhalo_ref[1, c, pl.ds(z, 1), :], (rx, ry))
            xl = jnp.where(first_x, g, xl)
            xh = jnp.where(last_x, g, xh)
            left = jnp.where(x_ids == 0, xl, pltpu.roll(g, 1, 0))
            right = jnp.where(x_ids == rx - 1, xh, pltpu.roll(g, rx - 1, 0))
            down = jnp.where(lane_ids == 0, g, pltpu.roll(g, 1, 1))
            up = jnp.where(lane_ids == ry - 1, g, pltpu.roll(g, ry - 1, 1))
            smooth = (g - below) + (g - above) + (g - left) + (g - right) + (g - down) + (g - up)
            grad_ref[c, z] = (2.0 * TV_WEIGHT) * smooth

    row_ids16 = row_ids
    for j in range(chunks):
        for d in range(1, ns):
            part_wait(d, j)
        at = pl.ds(j * chunk, chunk)
        front_c = jnp.zeros((3, chunk), jnp.float32)
        front_t = jnp.ones((1, chunk), jnp.float32)
        beyond = jnp.full((3, chunk), BACKGROUND, jnp.float32)
        for s in range(ns - 1):
            here = slab > s
            pc = parts_ref[s, j, pl.ds(0, 3), :]
            pt = parts_ref[s, j, pl.ds(3, 1), :]
            front_c = jnp.where(here, front_c + front_t * pc, front_c)
            front_t = jnp.where(here, front_t * pt, front_t)
        for s in range(ns - 1, 0, -1):
            here = slab < s
            pc = parts_ref[s, j, pl.ds(0, 3), :]
            pt = parts_ref[s, j, pl.ds(3, 1), :]
            beyond = jnp.where(here, pc + pt * beyond, beyond)
        pc = parts_ref[slab, j, pl.ds(0, 3), :]
        pt = parts_ref[slab, j, pl.ds(3, 1), :]
        rendered = front_c + front_t * (pc + pt * beyond)
        residual = RENDER_WEIGHT * (rendered - target_ref[:, at])
        color_cot = front_t * residual
        trans_cot = front_t * jnp.sum(residual * beyond, axis=0, keepdims=True)
        hot = onehot_ref[:, at]
        mask = row_ids16 == row_ref[:, at]
        for c in range(4):
            cot = color_cot[c:c + 1] if c < 3 else trans_cot
            spread = jnp.where(mask, cot, 0.0)
            top = spread.astype(jnp.bfloat16)
            rest = (spread - top.astype(jnp.float32)).astype(jnp.bfloat16)
            dims = (((1,), (1,)), ((), ()))
            u = lax.dot_general(top, hot, dims, preferred_element_type=jnp.float32)
            u = u + lax.dot_general(rest, hot, dims, preferred_element_type=jnp.float32)
            block = pl.ds(c * rows, rows)
            if j == 0:
                table_ref[block, :] = u
            else:
                table_ref[block, :] += u

    zero = jnp.zeros((rx, ry), jnp.float32)
    suffix = [zero, zero, zero]
    later = zero
    squares = zero
    for z in range(depth - 1, -1, -1):
        w = weight_ref[z]
        after = trans_ref[z]
        later = later + after * table_ref[pl.ds(3 * rows + z * rx, rx), :]
        dw = zero
        for c in range(3):
            suffix[c] = suffix[c] + table_ref[pl.ds(c * rows + z * rx, rx), :]
            col = sig_ref[c + 1, z]
            dw = dw + col * suffix[c]
            out = grad_ref[c + 1, z] + w * suffix[c] * (col * (1.0 - col))
            grad_ref[c + 1, z] = out
            squares = squares + out * out
        dtau = after * dw - later
        later = later + w * dw
        out = grad_ref[0, z] + dtau * (sig_ref[0, z] * span)
        grad_ref[0, z] = out
        squares = squares + out * out

    local = jnp.sum(squares)

    def norm_copy(phase, d, slot, peer):
        return pltpu.make_async_remote_copy(
            src_ref=nsend_ref.at[phase], dst_ref=nrecv_ref.at[slot],
            send_sem=norm_send.at[slot], recv_sem=norm_recv.at[slot],
            device_id=peer, device_id_type=MESH)

    value = jnp.full((8, 128), local, jnp.float32)
    copies = []
    for phase, count, peer in ((0, nt, tile_peer), (1, ns, slab_peer)):
        nsend_ref[phase] = value
        base = 0 if phase == 0 else nt - 1
        group = [norm_copy(phase, d, base + d - 1, peer(d)) for d in range(1, count)]
        for copy in group:
            copy.start()
        for i, copy in enumerate(group):
            copy.wait_recv()
            value = value + nrecv_ref[base + i]
        copies += group
    norm_ref[...] = value
    for copy in copies:
        copy.wait_send()
    for h in halos:
        h.wait_send()
    for j in range(chunks):
        for d in range(1, ns):
            part_copy(d, j).wait_send()


def per_device(voxel_grid, first_moment, second_moment, pixel_index, start_slab, ray_count, target):
    ns = lax.axis_size("slab")
    nt = lax.axis_size("tile")
    channels, depth, rx, ry = voxel_grid.shape
    rays = pixel_index.shape[0]
    chunk = math.gcd(rays, CHUNK)
    chunks = rays // chunk
    rows = depth * rx
    f32 = jnp.float32
    vmem = pl.BlockSpec(memory_space=pltpu.VMEM)
    gradient, square_sum = pl.pallas_call(
        functools.partial(kernel, ns, nt, chunk),
        out_shape=(
            jax.ShapeDtypeStruct(voxel_grid.shape, f32),
            jax.ShapeDtypeStruct((8, 128), f32),
        ),
        in_specs=[vmem] * 5,
        out_specs=(vmem, vmem),
        scratch_shapes=[
            pltpu.VMEM((channels * rows, ry), jnp.bfloat16),
            pltpu.VMEM((channels * rows, ry), jnp.bfloat16),
            pltpu.VMEM((depth, rx, ry), f32),
            pltpu.VMEM((depth, rx, ry), f32),
            pltpu.VMEM((channels, depth, rx, ry), f32),
            pltpu.VMEM((ry, rays), jnp.bfloat16),
            pltpu.VMEM((1, rays), jnp.int32),
            pltpu.VMEM((ns, chunks, 4, chunk), f32),
            pltpu.VMEM((channels * rows, ry), f32),
            pltpu.VMEM((2, channels, depth, ry), f32),
            pltpu.VMEM((2, channels, depth, ry), f32),
            pltpu.VMEM((2, channels, rx, ry), f32),
            pltpu.VMEM((2, 8, 128), f32),
            pltpu.VMEM((nt + ns - 2, 8, 128), f32),
            pltpu.SemaphoreType.DMA((ns - 1, chunks)),
            pltpu.SemaphoreType.DMA((ns - 1, chunks)),
            pltpu.SemaphoreType.DMA((4,)),
            pltpu.SemaphoreType.DMA((4,)),
            pltpu.SemaphoreType.DMA((nt + ns - 2,)),
            pltpu.SemaphoreType.DMA((nt + ns - 2,)),
        ],
        compiler_params=pltpu.CompilerParams(
            collective_id=0, has_side_effects=True, vmem_limit_bytes=32 * 1024 * 1024
        ),
        name="render_step",
    )(
        voxel_grid,
        pixel_index.reshape(1, rays),
        start_slab.reshape(1, rays),
        ray_count.reshape(1, rays),
        target,
    )
    norm_value = jnp.sqrt(square_sum[0, 0])
    limit = CLIP_RMS * math.sqrt(4.0 * (depth * ns) * (rx * nt) * ry)
    clipped = gradient * (limit / jnp.maximum(norm_value, limit))
    new_first = BETA_ONE * first_moment + (1.0 - BETA_ONE) * clipped
    new_second = BETA_TWO * second_moment + (1.0 - BETA_TWO) * clipped * clipped
    first_hat = new_first / (1.0 - BETA_ONE**STEP)
    second_hat = new_second / (1.0 - BETA_TWO**STEP)
    new_grid = voxel_grid - LEARN_RATE * first_hat / (jnp.sqrt(second_hat) + EPSILON)
    return (new_grid, new_first, new_second)


def solution(mesh):
    cells = P(None, "slab", "tile", None)
    return jax.shard_map(
        per_device,
        mesh=mesh,
        in_specs=(cells, cells, cells, P("tile"), P("tile"), P("tile"), P(None, "tile")),
        out_specs=(cells, cells, cells),
        check_vma=False,
    )
```

time: 175 us -> 34.9 us (0.20)
  blocking collectives: 71.7 us -> 0 us
  matrix products: 57.4 us -> 0 us
  Pallas kernels: 0 us -> 26.1 us
  other arithmetic: 25.5 us -> 2.4 us
  starting transfers between devices: 8.83 us -> 0 us
  waiting for transfers between devices: 3.45 us -> 0 us
    dot_general x10 -> x0, matrix products: 57.4 us -> none  [the longest x8 54.2 us: pick_block(): jnp.dot(flat, selector, precision=lax.Precision.HIGHEST, preferred_elemen...]
    psum x1 -> x0, blocking collectives: 43.4 us -> none  [per_device(): square_sum = lax.psum(jnp.sum(gradient * gradient), ('slab', 'tile'))]
    all_gather x2 -> x0, blocking collectives: 28.3 us -> none  [carried_in(): gathered = jax.tree.map(lambda a: lax.all_gather(a, axis), part)]
    pallas_call x0 -> x1, Pallas kernels: none -> 26.1 us  [per_device(): pl.pallas_call(functools.partial(kernel, ns, nt, chunk), out_shape=(jax.S...]
    dynamic_update_slice x4 -> x0, other arithmetic: 17.8 us -> none  [march_slab(): picked = lax.map(pick_block, pixel_blocks)]
    ppermute x4 -> x0, starting transfers between devices: 8.83 us -> none  [the longest x2 6.24 us: padded_2(): lax.ppermute(tail, axis, [(i, (i + 1) % count) for i in range(ends)])]
    ppermute x4 -> x0, waiting for transfers between devices: 3.45 us -> none  [the longest x2 3.45 us: padded_2(): lax.ppermute(head, axis, [((i + 1) % count, i) for i in range(ends)])]
    unnamed x18 -> x12, local copies, waits for them, and re-layouts: 1.5 us -> 4.03 us
  transfers between devices with their start and end apart: 4 -> 0, of which waited for: 1 -> 0; matrix products, arithmetic and copies ran while one was open for 48% -> 0% of each run, Pallas kernels for 0% -> 0%
where the time goes in v1:
time: 34.9 us; the launch traced here: 34.4 us
  Pallas kernels  26.1 us (75%)
  local copies, waits for them, and re-layouts  4.54 us (13%)
  other arithmetic  2.4 us (7%)
  between operations  1.39 us (4%)
    pallas_call x1, Pallas kernels, per_device(): pl.pallas_call(functools.partial(kernel, ns, nt, chunk), out_shape=(jax.S...  26.1 us
    unnamed x12, local copies, waits for them, and re-layouts  4.03 us
    sub x1, other arithmetic, per_device(): voxel_grid - LEARN_RATE * first_hat / (jnp.sqrt(second_hat) + EPSILON)  2.4 us

profile of v1, /device:TPU:0, one launch (start us, length us, event | category | flops | bytes accessed | tf_op | source)
XLA Modules:
  0.0 34.4 jit_solution(7303014829505646017)
XLA Ops:
  0.6 0.0 copy-start
  0.6 1.0 %copy-done = f32[4,16,8,256]{3,2,1,0:T(8,128)S(1)} copy-done((f32[4,16,8,256]{3,2,1,0:T(8,128)S(1)}, f32[4,16,8,256]{3,2,1,0:T(8,128)}, u32[]{:S(2)}) %copy-start) | copy-done | bytes 524312
  1.7 0.0 copy-start.1
  1.7 0.8 %copy-done.1 = f32[3,4096]{1,0:T(4,128)S(1)} copy-done((f32[3,4096]{1,0:T(4,128)S(1)}, f32[3,4096]{1,0:T(4,128)}, u32[]{:S(2)}) %copy-start.1) | copy-done | bytes 49176
  2.5 0.0 copy-start.2
  2.5 0.7 %copy-done.2 = s32[4096]{0:T(1024)S(1)} copy-done((s32[4096]{0:T(1024)S(1)}, s32[4096]{0:T(1024)}, u32[]{:S(2)}) %copy-start.2) | copy-done | bytes 16408
  3.2 0.0 copy-start.3
  3.2 0.7 %copy-done.3 = s32[4096]{0:T(1024)S(1)} copy-done((s32[4096]{0:T(1024)S(1)}, s32[4096]{0:T(1024)}, u32[]{:S(2)}) %copy-start.3) | copy-done | bytes 16408
  4.0 0.0 copy-start.4
  4.0 0.7 %copy-done.4 = s32[4096]{0:T(1024)S(1)} copy-done((s32[4096]{0:T(1024)S(1)}, s32[4096]{0:T(1024)}, u32[]{:S(2)}) %copy-start.4) | copy-done | bytes 16408
  4.7 0.0 copy-start.5
  4.7 26.1 %render_step.1 = (f32[4,16,8,256]{3,2,1,0:T(8,128)S(1)}, f32[8,128]{1,0:T(8,128)S(1)}) custom-call(f32[4,16,8,256]{3,2,1,0:T(8,128)S(1)} %copy-done, s32[1,4096]{1,0:T(1,128)S(1)} %bitcast.4, s32[1,4096]{1,0:T(1,128)S(1)} %bitcast.5, s32[1,4096]{1,0:T(1,128)S(1)} %bitcast.6, f32[3,4096]{1,0:T(4,128)S(1)} %copy-done.1), custom_call_target="tpu_custom_call" | custom-call | tf_op jit(solution)/shard_map/render_step/pallas_call | solution.py:277
  30.8 0.5 %slice.3 = f32[1,1]{1,0:T(1,128)} slice(f32[8,128]{1,0:T(8,128)S(1)} %get-tuple-element.6), slice={[0:1], [0:1]} | slice | bytes 8 | tf_op jit(solution)/shard_map/slice | solution.py:318
  32.0 0.0 copy-done.5
  32.0 2.4 %divide_subtract_fusion = (f32[4,16,8,256]{3,2,1,0:T(8,128)}, f32[4,16,8,256]{3,2,1,0:T(8,128)}, f32[4,16,8,256]{3,2,1,0:T(8,128)}) fusion(f32[4,16,8,256]{3,2,1,0:T(8,128)S(1)} %copy-done, f32[4,16,8,256]{3,2,1,0:T(8,128)S(1)} %get-tuple-element.5, f32[]{:T(128)} %bitcast.3, f32[4,16,8,256]{3,2,1,0:T(8,128)S(1)} %copy-done.5, f32[4,16,8,256]{3,2,1,0:T(8,128)} %param.9), kind=kLoop, calls=%fused_computation.2 | loop fusion | flops 1703936 | bytes 3670020 | tf_op jit(solution)/shard_map/sub | solution.py:325
Async XLA Ops:
  0.6 1.0 %copy-start = (f32[4,16,8,256]{3,2,1,0:T(8,128)S(1)}, f32[4,16,8,256]{3,2,1,0:T(8,128)}, u32[]{:S(2)}) copy-start(f32[4,16,8,256]{3,2,1,0:T(8,128)} %grid_ref.1) | copy-start | bytes 1572868
  1.7 0.8 %copy-start.1 = (f32[3,4096]{1,0:T(4,128)S(1)}, f32[3,4096]{1,0:T(4,128)}, u32[]{:S(2)}) copy-start(f32[3,4096]{1,0:T(4,128)} %target_ref.1) | copy-start | bytes 147460
  2.5 0.7 %copy-start.2 = (s32[4096]{0:T(1024)S(1)}, s32[4096]{0:T(1024)}, u32[]{:S(2)}) copy-start(s32[4096]{0:T(1024)} %param.10) | copy-start | bytes 49156
  3.2 0.7 %copy-start.3 = (s32[4096]{0:T(1024)S(1)}, s32[4096]{0:T(1024)}, u32[]{:S(2)}) copy-start(s32[4096]{0:T(1024)} %param.11) | copy-start | bytes 49156
  4.0 0.7 %copy-start.4 = (s32[4096]{0:T(1024)S(1)}, s32[4096]{0:T(1024)}, u32[]{:S(2)}) copy-start(s32[4096]{0:T(1024)} %param.12) | copy-start | bytes 49156
  4.7 27.3 %copy-start.5 = (f32[4,16,8,256]{3,2,1,0:T(8,128)S(1)}, f32[4,16,8,256]{3,2,1,0:T(8,128)}, u32[]{:S(2)}) copy-start(f32[4,16,8,256]{3,2,1,0:T(8,128)} %param.8) | copy-start | bytes 1572868

commit v2 on v1

--- a/solution.py
+++ b/solution.py
@@ -24,11 +24,12 @@
 
 def kernel(
     ns, nt, chunk,
-    grid_ref, pix_ref, start_ref, count_ref, target_ref,
-    grad_ref, norm_ref,
-    hi_ref, lo_ref, trans_ref, weight_ref, sig_ref, onehot_ref, row_ref, parts_ref, table_ref,
+    grid_hbm, first_hbm, second_hbm, pix_hbm, start_hbm, count_hbm, target_hbm,
+    grid_ref, first_ref, second_ref, grad_ref, scale_ref,
+    pix_ref, start_ref, count_ref, target_ref,
+    pair_ref, trans_ref, weight_ref, sig_ref, onehot_ref, row_ref, parts_ref, table_ref,
     edge_ref, xhalo_ref, zhalo_ref, nsend_ref, nrecv_ref,
-    part_send, part_recv, halo_send, halo_recv, norm_send, norm_recv,
+    part_send, part_recv, halo_send, halo_recv, norm_send, norm_recv, load_sem,
 ):
     channels, depth, rx, ry = grid_ref.shape
     rays = pix_ref.shape[1]
@@ -45,12 +46,28 @@
     def tile_peer(d):
         return {"tile": lax.rem(tile + d, nt)}
 
+    loads = [
+        pltpu.make_async_copy(grid_hbm.at[c], grid_ref.at[c], load_sem.at[c])
+        for c in range(channels)
+    ]
+    rest = (
+        (pix_hbm, pix_ref), (start_hbm, start_ref), (count_hbm, count_ref),
+        (target_hbm, target_ref), (first_hbm, first_ref), (second_hbm, second_ref),
+    )
+    loads += [
+        pltpu.make_async_copy(a, b, load_sem.at[channels + i]) for i, (a, b) in enumerate(rest)
+    ]
+    for copy in loads:
+        copy.start()
+
     barrier = pltpu.get_barrier_semaphore()
     for d in range(1, ns):
         pl.semaphore_signal(barrier, inc=1, device_id=slab_peer(d), device_id_type=MESH)
     for d in range(1, nt):
         pl.semaphore_signal(barrier, inc=1, device_id=tile_peer(d), device_id_type=MESH)
 
+    for c in range(channels):
+        loads[c].wait()
     edge_ref[0] = grid_ref[:, :, rx - 1, :]
     edge_ref[1] = grid_ref[:, :, 0, :]
 
@@ -76,29 +93,24 @@
         table_ref[pl.ds(3 * rows + z * rx, rx), :] = after
     full = table_ref[...]
     high = full.astype(jnp.bfloat16)
-    hi_ref[...] = high
-    lo_ref[...] = (full - high.astype(jnp.float32)).astype(jnp.bfloat16)
+    pair_ref[:, :ry] = high
+    pair_ref[:, ry:] = (full - high.astype(jnp.float32)).astype(jnp.bfloat16)
 
     pl.semaphore_wait(barrier, ns - 1 + nt - 1)
 
+    def halo_copy(src, dst, i, peer):
+        return pltpu.make_async_remote_copy(
+            src_ref=src, dst_ref=dst, send_sem=halo_send.at[i], recv_sem=halo_recv.at[i],
+            device_id=peer, device_id_type=MESH)
+
     halos = [
-        pltpu.make_async_remote_copy(
-            src_ref=grid_ref.at[:, depth - 1], dst_ref=zhalo_ref.at[0],
-            send_sem=halo_send.at[0], recv_sem=halo_recv.at[0],
-            device_id=slab_peer(1), device_id_type=MESH),
-        pltpu.make_async_remote_copy(
-            src_ref=grid_ref.at[:, 0], dst_ref=zhalo_ref.at[1],
-            send_sem=halo_send.at[1], recv_sem=halo_recv.at[1],
-            device_id=slab_peer(ns - 1), device_id_type=MESH),
-        pltpu.make_async_remote_copy(
-            src_ref=edge_ref.at[0], dst_ref=xhalo_ref.at[0],
-            send_sem=halo_send.at[2], recv_sem=halo_recv.at[2],
-            device_id=tile_peer(1), device_id_type=MESH),
-        pltpu.make_async_remote_copy(
-            src_ref=edge_ref.at[1], dst_ref=xhalo_ref.at[1],
-            send_sem=halo_send.at[3], recv_sem=halo_recv.at[3],
-            device_id=tile_peer(nt - 1), device_id_type=MESH),
+        (halo_copy(grid_ref.at[:, depth - 1], zhalo_ref.at[0], 0, slab_peer(1)), slab < ns - 1, slab > 0),
+        (halo_copy(grid_ref.at[:, 0], zhalo_ref.at[1], 1, slab_peer(ns - 1)), slab > 0, slab < ns - 1),
+        (halo_copy(edge_ref.at[0], xhalo_ref.at[0], 2, tile_peer(1)), tile < nt - 1, tile > 0),
+        (halo_copy(edge_ref.at[1], xhalo_ref.at[1], 3, tile_peer(nt - 1)), tile > 0, tile < nt - 1),
     ]
+    for copy, sends, _ in halos:
+        pl.when(sends)(copy.start)
 
     def part_copy(d, j):
         return pltpu.make_async_remote_copy(
@@ -116,6 +128,8 @@
     y_ids = lax.broadcasted_iota(jnp.int32, (ry, chunk), 0).astype(jnp.float32).astype(jnp.bfloat16)
     row_ids = lax.broadcasted_iota(jnp.int32, (rows, chunk), 0)
 
+    for copy in loads[channels:channels + 3]:
+        copy.wait()
     for j in range(chunks):
         at = pl.ds(j * chunk, chunk)
         pix = pix_ref[:, at]
@@ -128,23 +142,20 @@
         row_ref[:, at] = row
         hot = jnp.where(y_ids == py, jnp.ones((), jnp.bfloat16), jnp.zeros((), jnp.bfloat16))
         onehot_ref[:, at] = hot
+        twice = jnp.concatenate([hot, hot], axis=0)
         mask = row_ids == row
         for c in range(4):
             block = pl.ds(c * rows, rows)
-            u = jnp.dot(hi_ref[block, :], hot, preferred_element_type=jnp.float32)
-            u = u + jnp.dot(lo_ref[block, :], hot, preferred_element_type=jnp.float32)
+            u = jnp.dot(pair_ref[block, :], twice, preferred_element_type=jnp.float32)
             part = jnp.sum(jnp.where(mask, u, 0.0), axis=0, keepdims=True)
             if c == 3:
                 part = jnp.where(row < 0, 1.0, part)
             parts_ref[slab, j, pl.ds(c, 1), :] = part
         for d in range(1, ns):
             part_copy(d, j).start()
-        if j == 0:
-            for h in halos:
-                h.start()
-
-    for h in halos:
-        h.wait_recv()
+
+    for copy, _, receives in halos:
+        pl.when(receives)(copy.wait_recv)
     x_ids = lax.broadcasted_iota(jnp.int32, (rx, ry), 0)
     lane_ids = lax.broadcasted_iota(jnp.int32, (rx, ry), 1)
     first_x = tile == 0
@@ -171,7 +182,8 @@
             smooth = (g - below) + (g - above) + (g - left) + (g - right) + (g - down) + (g - up)
             grad_ref[c, z] = (2.0 * TV_WEIGHT) * smooth
 
-    row_ids16 = row_ids
+    loads[channels + 3].wait()
+    row_ids16 = row_ids.astype(jnp.float32).astype(jnp.bfloat16)
     for j in range(chunks):
         for d in range(1, ns):
             part_wait(d, j)
@@ -197,15 +209,17 @@
         color_cot = front_t * residual
         trans_cot = front_t * jnp.sum(residual * beyond, axis=0, keepdims=True)
         hot = onehot_ref[:, at]
-        mask = row_ids16 == row_ref[:, at]
+        twice = jnp.concatenate([hot, hot], axis=1)
+        mask = row_ids16 == row_ref[:, at].astype(jnp.float32).astype(jnp.bfloat16)
+        none = jnp.zeros((), jnp.bfloat16)
         for c in range(4):
             cot = color_cot[c:c + 1] if c < 3 else trans_cot
-            spread = jnp.where(mask, cot, 0.0)
-            top = spread.astype(jnp.bfloat16)
-            rest = (spread - top.astype(jnp.float32)).astype(jnp.bfloat16)
-            dims = (((1,), (1,)), ((), ()))
-            u = lax.dot_general(top, hot, dims, preferred_element_type=jnp.float32)
-            u = u + lax.dot_general(rest, hot, dims, preferred_element_type=jnp.float32)
+            top = cot.astype(jnp.bfloat16)
+            low = (cot - top.astype(jnp.float32)).astype(jnp.bfloat16)
+            spread = jnp.concatenate(
+                [jnp.where(mask, top, none), jnp.where(mask, low, none)], axis=1)
+            u = lax.dot_general(
+                spread, twice, (((1,), (1,)), ((), ())), preferred_element_type=jnp.float32)
             block = pl.ds(c * rows, rows)
             if j == 0:
                 table_ref[block, :] = u
@@ -254,14 +268,44 @@
             copy.wait_recv()
             value = value + nrecv_ref[base + i]
         copies += group
-    norm_ref[...] = value
+    limit = CLIP_RMS * math.sqrt(4.0 * total_depth * (rx * nt) * ry)
+    scale_ref[...] = limit / jnp.maximum(jnp.sqrt(value), limit)
+    for copy in loads[channels + 4:]:
+        copy.wait()
     for copy in copies:
         copy.wait_send()
-    for h in halos:
-        h.wait_send()
+    for copy, sends, _ in halos:
+        pl.when(sends)(copy.wait_send)
     for j in range(chunks):
         for d in range(1, ns):
             part_copy(d, j).wait_send()
+
+
+def adam_kernel(
+    grid_ref, first_ref, second_ref, grad_ref, scale_ref,
+    grid_hbm, first_hbm, second_hbm, grid_out, first_out, second_out, sem,
+):
+    channels, depth, rx, ry = grid_ref.shape
+    scale = jnp.broadcast_to(scale_ref[0:1, 0:1], (rx, ry))
+    copies = []
+    for c in range(channels):
+        for z in range(depth):
+            clipped = grad_ref[c, z] * scale
+            first = BETA_ONE * first_ref[c, z] + (1.0 - BETA_ONE) * clipped
+            second = BETA_TWO * second_ref[c, z] + (1.0 - BETA_TWO) * clipped * clipped
+            first_out[c, z] = first
+            second_out[c, z] = second
+            first_hat = first * (1.0 / (1.0 - BETA_ONE**STEP))
+            second_hat = second * (1.0 / (1.0 - BETA_TWO**STEP))
+            grid_out[c, z] = grid_ref[c, z] - LEARN_RATE * first_hat / (
+                jnp.sqrt(second_hat) + EPSILON)
+        pairs = ((first_out, first_hbm), (second_out, second_hbm), (grid_out, grid_hbm))
+        for i, (a, b) in enumerate(pairs):
+            copy = pltpu.make_async_copy(a.at[c], b.at[c], sem.at[i, c])
+            copy.start()
+            copies.append(copy)
+    for copy in copies:
+        copy.wait()
 
 
 def per_device(voxel_grid, first_moment, second_moment, pixel_index, start_slab, ray_count, target):
@@ -274,17 +318,19 @@
     rows = depth * rx
     f32 = jnp.float32
     vmem = pl.BlockSpec(memory_space=pltpu.VMEM)
-    gradient, square_sum = pl.pallas_call(
+    hbm = pl.BlockSpec(memory_space=pltpu.HBM)
+    cells = jax.ShapeDtypeStruct(voxel_grid.shape, f32)
+    staged = pl.pallas_call(
         functools.partial(kernel, ns, nt, chunk),
-        out_shape=(
-            jax.ShapeDtypeStruct(voxel_grid.shape, f32),
-            jax.ShapeDtypeStruct((8, 128), f32),
-        ),
-        in_specs=[vmem] * 5,
-        out_specs=(vmem, vmem),
+        out_shape=(cells, cells, cells, cells, jax.ShapeDtypeStruct((8, 128), f32)),
+        in_specs=[hbm] * 7,
+        out_specs=(vmem,) * 5,
         scratch_shapes=[
-            pltpu.VMEM((channels * rows, ry), jnp.bfloat16),
-            pltpu.VMEM((channels * rows, ry), jnp.bfloat16),
+            pltpu.VMEM((1, rays), jnp.int32),
+            pltpu.VMEM((1, rays), jnp.int32),
+            pltpu.VMEM((1, rays), jnp.int32),
+            pltpu.VMEM(target.shape, f32),
+            pltpu.VMEM((channels * rows, 2 * ry), jnp.bfloat16),
             pltpu.VMEM((depth, rx, ry), f32),
             pltpu.VMEM((depth, rx, ry), f32),
             pltpu.VMEM((channels, depth, rx, ry), f32),
@@ -303,27 +349,35 @@
             pltpu.SemaphoreType.DMA((4,)),
             pltpu.SemaphoreType.DMA((nt + ns - 2,)),
             pltpu.SemaphoreType.DMA((nt + ns - 2,)),
+            pltpu.SemaphoreType.DMA((channels + 6,)),
         ],
         compiler_params=pltpu.CompilerParams(
             collective_id=0, has_side_effects=True, vmem_limit_bytes=32 * 1024 * 1024
         ),
         name="render_step",
-    )(
+    )(*(pltpu.with_memory_space_constraint(a, pltpu.HBM) for a in (
         voxel_grid,
+        first_moment,
+        second_moment,
         pixel_index.reshape(1, rays),
         start_slab.reshape(1, rays),
         ray_count.reshape(1, rays),
         target,
-    )
-    norm_value = jnp.sqrt(square_sum[0, 0])
-    limit = CLIP_RMS * math.sqrt(4.0 * (depth * ns) * (rx * nt) * ry)
-    clipped = gradient * (limit / jnp.maximum(norm_value, limit))
-    new_first = BETA_ONE * first_moment + (1.0 - BETA_ONE) * clipped
-    new_second = BETA_TWO * second_moment + (1.0 - BETA_TWO) * clipped * clipped
-    first_hat = new_first / (1.0 - BETA_ONE**STEP)
-    second_hat = new_second / (1.0 - BETA_TWO**STEP)
-    new_grid = voxel_grid - LEARN_RATE * first_hat / (jnp.sqrt(second_hat) + EPSILON)
-    return (new_grid, new_first, new_second)
+    )))
+    return pl.pallas_call(
+        adam_kernel,
+        out_shape=(cells, cells, cells),
+        in_specs=[vmem] * 5,
+        out_specs=(hbm, hbm, hbm),
+        scratch_shapes=[
+            pltpu.VMEM(voxel_grid.shape, f32),
+            pltpu.VMEM(voxel_grid.shape, f32),
+            pltpu.VMEM(voxel_grid.shape, f32),
+            pltpu.SemaphoreType.DMA((3, channels)),
+        ],
+        compiler_params=pltpu.CompilerParams(vmem_limit_bytes=32 * 1024 * 1024),
+        name="adam",
+    )(*staged)
 
 
 def solution(mesh):

time: 34.9 us -> 26.4 us (0.76); the launches traced: 34.4 us -> 26.3 us
  local copies, waits for them, and re-layouts: 4.54 us -> 0 us
  other arithmetic: 2.4 us -> 0 us
  between operations: 1.39 us -> 0.64 us
  Pallas kernels: 26.1 us -> 25.7 us
    unnamed x12 -> x0, local copies, waits for them, and re-layouts: 4.03 us -> none
    sub x1 -> x0, other arithmetic: 2.4 us -> none  [per_device(): voxel_grid - LEARN_RATE * first_hat / (jnp.sqrt(second_hat) + EPSILON)]
    slice x1 -> x0, local copies, waits for them, and re-layouts: 0.51 us -> none  [per_device(): norm_value = jnp.sqrt(square_sum[0, 0])]
    pallas_call x1 -> x2, Pallas kernels: 26.1 us -> 25.7 us  [the longest x1 24.3 us: per_device(): pl.pallas_call(functools.partial(kernel, ns, nt, chunk), out_shape=(cells...]
where the time goes in v2:
time: 26.4 us; the launch traced here: 26.3 us
  Pallas kernels  25.7 us (97%)
  between operations  0.64 us (2%)
    pallas_call x1, Pallas kernels, per_device(): pl.pallas_call(functools.partial(kernel, ns, nt, chunk), out_shape=(cells...  24.3 us
    pallas_call x1, Pallas kernels, per_device(): pl.pallas_call(adam_kernel, out_shape=(cells, cells, cells), in_specs=[vm...  1.35 us

profile of v2, /device:TPU:0, one launch (start us, length us, event | category | flops | bytes accessed | tf_op | source)
XLA Modules:
  0.0 26.3 jit_solution(10684828417392472519)
XLA Ops:
  0.6 24.3 %render_step.1 = (f32[4,16,8,256]{3,2,1,0:T(8,128)S(1)}, f32[4,16,8,256]{3,2,1,0:T(8,128)S(1)}, f32[4,16,8,256]{3,2,1,0:T(8,128)S(1)}, f32[4,16,8,256]{3,2,1,0:T(8,128)S(1)}, f32[8,128]{1,0:T(8,128)S(1)}) custom-call(f32[4,16,8,256]{3,2,1,0:T(8,128)} %grid_hbm.1, f32[4,16,8,256]{3,2,1,0:T(8,128)} %first_hbm.1, f32[4,16,8,256]{3,2,1,0:T(8,128)} %second_hbm.1, ...), custom_call_target="tpu_custom_call" | custom-call | tf_op jit(solution)/shard_map/render_step/pallas_call | solution.py:323
  24.9 1.4 %adam.1 = (f32[4,16,8,256]{3,2,1,0:T(8,128)}, f32[4,16,8,256]{3,2,1,0:T(8,128)}, f32[4,16,8,256]{3,2,1,0:T(8,128)}) custom-call(f32[4,16,8,256]{3,2,1,0:T(8,128)S(1)} %get-tuple-element.8.grid_ref, f32[4,16,8,256]{3,2,1,0:T(8,128)S(1)} %get-tuple-element.9.first_ref, f32[4,16,8,256]{3,2,1,0:T(8,128)S(1)} %get-tuple-element.10.second_ref, ...), custom_call_target="tpu_custom_call" | custom-call | tf_op jit(solution)/shard_map/adam/pallas_call | solution.py:367

commit v3 on v2

--- a/solution.py
+++ b/solution.py
@@ -18,7 +18,8 @@
 BETA_ONE = 0.9
 BETA_TWO = 0.99
 EPSILON = 1e-08
-CHUNK = 1024
+CHUNK = 512
+DIRECT_LIMIT = 64
 MESH = pl.DeviceIdType.MESH
 
 
@@ -46,6 +47,16 @@
     def tile_peer(d):
         return {"tile": lax.rem(tile + d, nt)}
 
+    if direct(ns, nt):
+        phases = [[
+            {"slab": lax.rem(slab + k // nt, ns), "tile": lax.rem(tile + k % nt, nt)}
+            for k in range(1, ns * nt)
+        ]]
+        greeted = phases[0]
+    else:
+        phases = [[tile_peer(d) for d in range(1, nt)], [slab_peer(d) for d in range(1, ns)]]
+        greeted = phases[0] + phases[1]
+
     loads = [
         pltpu.make_async_copy(grid_hbm.at[c], grid_ref.at[c], load_sem.at[c])
         for c in range(channels)
@@ -61,10 +72,8 @@
         copy.start()
 
     barrier = pltpu.get_barrier_semaphore()
-    for d in range(1, ns):
-        pl.semaphore_signal(barrier, inc=1, device_id=slab_peer(d), device_id_type=MESH)
-    for d in range(1, nt):
-        pl.semaphore_signal(barrier, inc=1, device_id=tile_peer(d), device_id_type=MESH)
+    for peer in greeted:
+        pl.semaphore_signal(barrier, inc=1, device_id=peer, device_id_type=MESH)
 
     for c in range(channels):
         loads[c].wait()
@@ -96,7 +105,7 @@
     pair_ref[:, :ry] = high
     pair_ref[:, ry:] = (full - high.astype(jnp.float32)).astype(jnp.bfloat16)
 
-    pl.semaphore_wait(barrier, ns - 1 + nt - 1)
+    pl.semaphore_wait(barrier, len(greeted))
 
     def halo_copy(src, dst, i, peer):
         return pltpu.make_async_remote_copy(
@@ -250,23 +259,24 @@
 
     local = jnp.sum(squares)
 
-    def norm_copy(phase, d, slot, peer):
+    def norm_copy(phase, slot, peer):
         return pltpu.make_async_remote_copy(
             src_ref=nsend_ref.at[phase], dst_ref=nrecv_ref.at[slot],
             send_sem=norm_send.at[slot], recv_sem=norm_recv.at[slot],
             device_id=peer, device_id_type=MESH)
 
-    value = jnp.full((8, 128), local, jnp.float32)
+    value = jnp.full((1, 128), local, jnp.float32)
     copies = []
-    for phase, count, peer in ((0, nt, tile_peer), (1, ns, slab_peer)):
+    base = 0
+    for phase, peers in enumerate(phases):
         nsend_ref[phase] = value
-        base = 0 if phase == 0 else nt - 1
-        group = [norm_copy(phase, d, base + d - 1, peer(d)) for d in range(1, count)]
+        group = [norm_copy(phase, base + i, peer) for i, peer in enumerate(peers)]
         for copy in group:
             copy.start()
         for i, copy in enumerate(group):
             copy.wait_recv()
             value = value + nrecv_ref[base + i]
+        base += len(group)
         copies += group
     limit = CLIP_RMS * math.sqrt(4.0 * total_depth * (rx * nt) * ry)
     scale_ref[...] = limit / jnp.maximum(jnp.sqrt(value), limit)
@@ -279,6 +289,10 @@
     for j in range(chunks):
         for d in range(1, ns):
             part_copy(d, j).wait_send()
+
+
+def direct(ns, nt):
+    return ns * nt <= DIRECT_LIMIT
 
 
 def adam_kernel(
@@ -316,13 +330,14 @@
     chunk = math.gcd(rays, CHUNK)
     chunks = rays // chunk
     rows = depth * rx
+    messages = ns * nt - 1 if direct(ns, nt) else nt + ns - 2
     f32 = jnp.float32
     vmem = pl.BlockSpec(memory_space=pltpu.VMEM)
     hbm = pl.BlockSpec(memory_space=pltpu.HBM)
     cells = jax.ShapeDtypeStruct(voxel_grid.shape, f32)
     staged = pl.pallas_call(
         functools.partial(kernel, ns, nt, chunk),
-        out_shape=(cells, cells, cells, cells, jax.ShapeDtypeStruct((8, 128), f32)),
+        out_shape=(cells, cells, cells, cells, jax.ShapeDtypeStruct((1, 128), f32)),
         in_specs=[hbm] * 7,
         out_specs=(vmem,) * 5,
         scratch_shapes=[
@@ -341,14 +356,14 @@
             pltpu.VMEM((2, channels, depth, ry), f32),
             pltpu.VMEM((2, channels, depth, ry), f32),
             pltpu.VMEM((2, channels, rx, ry), f32),
-            pltpu.VMEM((2, 8, 128), f32),
-            pltpu.VMEM((nt + ns - 2, 8, 128), f32),
+            pltpu.VMEM((2, 1, 128), f32),
+            pltpu.VMEM((messages, 1, 128), f32),
             pltpu.SemaphoreType.DMA((ns - 1, chunks)),
             pltpu.SemaphoreType.DMA((ns - 1, chunks)),
             pltpu.SemaphoreType.DMA((4,)),
             pltpu.SemaphoreType.DMA((4,)),
-            pltpu.SemaphoreType.DMA((nt + ns - 2,)),
-            pltpu.SemaphoreType.DMA((nt + ns - 2,)),
+            pltpu.SemaphoreType.DMA((messages,)),
+            pltpu.SemaphoreType.DMA((messages,)),
             pltpu.SemaphoreType.DMA((channels + 6,)),
         ],
         compiler_params=pltpu.CompilerParams(

time: 26.4 us -> 24.6 us (0.932)
  Pallas kernels: 25.7 us -> 23.8 us
    pallas_call x1, Pallas kernels: 24.3 us -> 22.4 us  [per_device(): pl.pallas_call(functools.partial(kernel, ns, nt, chunk), out_shape=(cells...]
where the time goes in v3:
time: 24.6 us; the launch traced here: 24.4 us
  Pallas kernels  23.8 us (97%)
  between operations  0.64 us (3%)
    pallas_call x1, Pallas kernels, per_device(): pl.pallas_call(functools.partial(kernel, ns, nt, chunk), out_shape=(cells...  22.4 us
    pallas_call x1, Pallas kernels, per_device(): pl.pallas_call(adam_kernel, out_shape=(cells, cells, cells), in_specs=[vm...  1.39 us

profile of v3, /device:TPU:0, one launch (start us, length us, event | category | flops | bytes accessed | tf_op | source)
XLA Modules:
  0.0 24.4 jit_solution(9349233033911594734)
XLA Ops:
  0.6 22.4 %render_step.1 = (f32[4,16,8,256]{3,2,1,0:T(8,128)S(1)}, f32[4,16,8,256]{3,2,1,0:T(8,128)S(1)}, f32[4,16,8,256]{3,2,1,0:T(8,128)S(1)}, f32[4,16,8,256]{3,2,1,0:T(8,128)S(1)}, f32[1,128]{1,0:T(1,128)S(1)}) custom-call(f32[4,16,8,256]{3,2,1,0:T(8,128)} %grid_hbm.1, f32[4,16,8,256]{3,2,1,0:T(8,128)} %first_hbm.1, f32[4,16,8,256]{3,2,1,0:T(8,128)} %second_hbm.1, ...), custom_call_target="tpu_custom_call" | custom-call | tf_op jit(solution)/shard_map/render_step/pallas_call | solution.py:338
  23.1 1.4 %adam.1 = (f32[4,16,8,256]{3,2,1,0:T(8,128)}, f32[4,16,8,256]{3,2,1,0:T(8,128)}, f32[4,16,8,256]{3,2,1,0:T(8,128)}) custom-call(f32[4,16,8,256]{3,2,1,0:T(8,128)S(1)} %get-tuple-element.8.grid_ref, f32[4,16,8,256]{3,2,1,0:T(8,128)S(1)} %get-tuple-element.9.first_ref, f32[4,16,8,256]{3,2,1,0:T(8,128)S(1)} %get-tuple-element.10.second_ref, ...), custom_call_target="tpu_custom_call" | custom-call | tf_op jit(solution)/shard_map/adam/pallas_call | solution.py:382

commit v4 on v3

--- a/solution.py
+++ b/solution.py
@@ -48,11 +48,15 @@
         return {"tile": lax.rem(tile + d, nt)}
 
     if direct(ns, nt):
-        phases = [[
-            {"slab": lax.rem(slab + k // nt, ns), "tile": lax.rem(tile + k % nt, nt)}
-            for k in range(1, ns * nt)
-        ]]
-        greeted = phases[0]
+        pair = {"tile": tile + 1 - 2 * lax.rem(tile, 2)}
+        half = nt // 2
+        others = [
+            {"slab": lax.rem(slab + k // half, ns), "tile": lax.rem(tile + 2 * (k % half), nt)}
+            for k in range(1, ns * half)
+        ]
+        phases = [[pair], others]
+        greeted = [pair] + [{"slab": lax.rem(slab + k // nt, ns), "tile": lax.rem(tile + k % nt, nt)} for k in range(1, ns * nt)]
+        greeted = greeted[1:]
     else:
         phases = [[tile_peer(d) for d in range(1, nt)], [slab_peer(d) for d in range(1, ns)]]
         greeted = phases[0] + phases[1]
@@ -292,7 +296,7 @@
 
 
 def direct(ns, nt):
-    return ns * nt <= DIRECT_LIMIT
+    return ns * nt <= DIRECT_LIMIT and nt % 2 == 0
 
 
 def adam_kernel(
@@ -330,7 +334,7 @@
     chunk = math.gcd(rays, CHUNK)
     chunks = rays // chunk
     rows = depth * rx
-    messages = ns * nt - 1 if direct(ns, nt) else nt + ns - 2
+    messages = ns * nt // 2 if direct(ns, nt) else nt + ns - 2
     f32 = jnp.float32
     vmem = pl.BlockSpec(memory_space=pltpu.VMEM)
     hbm = pl.BlockSpec(memory_space=pltpu.HBM)

time: 24.6 us -> 24.2 us (0.984)
  Pallas kernels: 23.8 us -> 23.5 us
    pallas_call x1, Pallas kernels: 22.4 us -> 22.1 us  [per_device(): pl.pallas_call(functools.partial(kernel, ns, nt, chunk), out_shape=(cells...]
where the time goes in v4:
time: 24.2 us; the launch traced here: 24.1 us
  Pallas kernels  23.5 us (97%)
  between operations  0.64 us (3%)
    pallas_call x1, Pallas kernels, per_device(): pl.pallas_call(functools.partial(kernel, ns, nt, chunk), out_shape=(cells...  22.1 us
    pallas_call x1, Pallas kernels, per_device(): pl.pallas_call(adam_kernel, out_shape=(cells, cells, cells), in_specs=[vm...  1.39 us

profile of v4, /device:TPU:0, one launch (start us, length us, event | category | flops | bytes accessed | tf_op | source)
XLA Modules:
  0.0 24.1 jit_solution(6045972008893178670)
XLA Ops:
  0.6 22.1 %render_step.1 = (f32[4,16,8,256]{3,2,1,0:T(8,128)S(1)}, f32[4,16,8,256]{3,2,1,0:T(8,128)S(1)}, f32[4,16,8,256]{3,2,1,0:T(8,128)S(1)}, f32[4,16,8,256]{3,2,1,0:T(8,128)S(1)}, f32[1,128]{1,0:T(1,128)S(1)}) custom-call(f32[4,16,8,256]{3,2,1,0:T(8,128)} %grid_hbm.1, f32[4,16,8,256]{3,2,1,0:T(8,128)} %first_hbm.1, f32[4,16,8,256]{3,2,1,0:T(8,128)} %second_hbm.1, ...), custom_call_target="tpu_custom_call" | custom-call | tf_op jit(solution)/shard_map/render_step/pallas_call | solution.py:342
  22.7 1.4 %adam.1 = (f32[4,16,8,256]{3,2,1,0:T(8,128)}, f32[4,16,8,256]{3,2,1,0:T(8,128)}, f32[4,16,8,256]{3,2,1,0:T(8,128)}) custom-call(f32[4,16,8,256]{3,2,1,0:T(8,128)S(1)} %get-tuple-element.8.grid_ref, f32[4,16,8,256]{3,2,1,0:T(8,128)S(1)} %get-tuple-element.9.first_ref, f32[4,16,8,256]{3,2,1,0:T(8,128)S(1)} %get-tuple-element.10.second_ref, ...), custom_call_target="tpu_custom_call" | custom-call | tf_op jit(solution)/shard_map/adam/pallas_call | solution.py:386
